TPU v7x, 32 devices: a whole 2x2x4 slice. The times are simulated.
32 devices in a mesh: groups: 2 (over x), rows: 8 (over z, y), cols: 2 (over core).
Axes of the slice: x: 2, y: 2, z: 4, core: 2. Of those that a mesh axis runs over, the one named last changes fastest.
Arguments:
- feature_table: float32 [32768, 1024], P(('groups', 'rows'), 'cols'), parts along dimension 0, may hold values from -6 to 6
- own_features: float32 [512, 1024], P(('groups', 'rows'), 'cols'), parts along dimension 0, may hold values from -6 to 6
- neighbor_ids: int32 [512, 50], P(('groups', 'rows')), parts along dimension 0, may hold values from 0 to 16383, as said below
- importance: float32 [512, 50], P(('groups', 'rows')), parts along dimension 0, may hold values from 0.5 to 5
- w_self: bfloat16 [1024, 1024], P('cols'), may hold values from -0.1875 to 0.1875
- w_pool: bfloat16 [1024, 1024], P('cols'), may hold values from -0.1875 to 0.1875
- bias: float32 [1024], replicated, may hold values from -6 to 6
Outputs:
- embeddings: float32 [512, 1024], P(('groups', 'rows'), 'cols'), parts along dimension 0
There are 2 independent parts, one for each index of `groups`. A program takes and returns all parts, laid end to end along the dimension named above; an argument that names none is the same for every part. Nothing has to cross between parts.
Inputs may be any that keep to these rules, and one draw needn't show every extreme that they name: `neighbor_ids`: ids of sampled neighbors in the group's table, repeats allowed. In each aligned block of 16 targets, at most 160 ids fall in any one range [k * 2048, (k + 1) * 2048), and one such range holds exactly 160.
All inputs are finite; a program needn't handle non-finite values.
Results may differ from a plain program's by a relative error of at most 0.0017.
Values may be sent and summed in bfloat16 or wider, within the bound.
A program may use at most 64 MiB of HBM per device.

v0:
```python
from functools import partial
import jax
import jax.numpy as jnp
from jax import lax
from jax.sharding import PartitionSpec as P

NEIGH = 50
TGT_DEV = 16


def request_slots(id_block, share_block, owners, capacity, rows_dev):
    targets = id_block.shape[0]
    neighbors = id_block.shape[1]
    flat_ids = id_block.reshape(-1)
    owner_of = flat_ids // rows_dev
    local_row = flat_ids - owner_of * rows_dev
    target_of = jnp.arange(targets * neighbors, dtype=jnp.int32) // neighbors
    onehot = (owner_of[:, None] == jnp.arange(owners, dtype=jnp.int32)[None, :]).astype(jnp.int32)
    slot_rank = jnp.sum((jnp.cumsum(onehot, axis=0) - onehot) * onehot, axis=1)
    sending = jnp.zeros((owners, capacity), jnp.int32).at[owner_of, slot_rank].set(local_row)
    packed = (
        jnp.zeros((owners, capacity), jnp.int32)
        .at[owner_of, slot_rank]
        .set(local_row * targets + target_of)
    )
    slot_weight = (
        jnp.zeros((owners, capacity), jnp.float32)
        .at[owner_of, slot_rank]
        .set(share_block.reshape(-1))
    )
    return (owner_of, slot_rank, sending, packed, slot_weight)


def plan_requests(id_rows, shares, blocks, owners, capacity, rows_dev):
    targets = id_rows.shape[0] // blocks
    neighbors = id_rows.shape[1]
    per_block = targets * neighbors
    owner_of, slot_rank, sending, packed, slot_weight = jax.vmap(
        partial(request_slots, owners=owners, capacity=capacity, rows_dev=rows_dev)
    )(id_rows.reshape(blocks, targets, neighbors), shares.reshape(blocks, targets, neighbors))
    block_of = jnp.arange(blocks, dtype=jnp.int32)[:, None]
    column = owner_of * (blocks * capacity) + block_of * capacity + slot_rank
    row_index = block_of * targets + jnp.arange(per_block, dtype=jnp.int32)[None, :] // neighbors
    pool_matrix = (
        jnp.zeros((blocks * targets, owners * blocks * capacity), jnp.float32)
        .at[row_index.reshape(-1), column.reshape(-1)]
        .add(shares.reshape(-1))
    )
    outgoing = jnp.transpose(sending, (1, 0, 2)).reshape(owners, blocks * capacity)
    packed_out = jnp.transpose(packed, (1, 0, 2)).reshape(owners, blocks * capacity)
    weight_out = jnp.transpose(slot_weight, (1, 0, 2)).reshape(owners, blocks * capacity)
    return (pool_matrix, outgoing, packed_out, weight_out)


def finish_rows(preact):
    hidden = jnp.maximum(preact, 0.0)
    return hidden * lax.rsqrt(jnp.mean(hidden * hidden, axis=1, keepdims=True) + 1e-06)


def body(feature_table, own_features, neighbor_ids, importance, w_self, w_pool, bias):
    rows_dev, width_half = feature_table.shape
    owners = lax.axis_size("rows")
    col_count = lax.axis_size("cols")
    capacity = TGT_DEV * NEIGH * 8 // (5 * owners)
    shares = importance / jnp.sum(importance, axis=1, keepdims=True)
    own_round = own_features.astype(jnp.bfloat16)
    pool_matrix, outgoing, packed_out, weight_out = plan_requests(
        neighbor_ids, shares, col_count, owners, capacity, rows_dev
    )
    found = jnp.take(
        feature_table,
        lax.all_to_all(outgoing, "rows", split_axis=0, concat_axis=0, tiled=True),
        axis=0,
    )
    arrived = lax.all_to_all(
        found.astype(jnp.bfloat16), "rows", split_axis=0, concat_axis=0, tiled=True
    ).astype(found.dtype)
    pooled = jnp.dot(
        pool_matrix,
        arrived.reshape(-1, width_half),
        precision=lax.Precision.HIGHEST,
        preferred_element_type=jnp.float32,
    )
    partial_sums = jnp.dot(own_round, w_self, preferred_element_type=jnp.float32) + jnp.dot(
        pooled.astype(jnp.bfloat16), w_pool, preferred_element_type=jnp.float32
    )
    column_start = lax.axis_index("cols") * width_half
    preact = lax.psum(partial_sums, "cols") + bias
    embedded = finish_rows(preact)
    return lax.dynamic_slice_in_dim(embedded, column_start, width_half, 1)


def solution(mesh):
    placed = (
        P(("groups", "rows"), "cols"),
        P(("groups", "rows"), "cols"),
        P(("groups", "rows"), None),
        P(("groups", "rows"), None),
        P("cols", None),
        P("cols", None),
        P(),
    )
    return jax.shard_map(
        body, mesh=mesh, in_specs=placed, out_specs=P(("groups", "rows"), "cols"), check_vma=False
    )
```

profile of v0, /device:TPU:0, one launch (start us, length us, event | category | flops | bytes accessed | tf_op | source)
XLA Modules:
  0.0 143.6 jit_solution(3626495202267903380)
XLA Ops:
  6.5 0.0 copy-start
  6.5 0.9 reshape_reshape.8
  7.4 0.8 reshape_reshape.9
  8.3 4.0 %reduce-window.6 = s32[2,8,7,128]{3,1,2,0:T(8,128)S(1)} reduce-window(s32[2,8,7,128]{3,1,2,0:T(8,128)S(1)} %convert_bitcast_fusion, s32[]{:T(128)} %constant.33.clone.1), window={size=1x1x1x128 pad=0_0x0_0x0_0x127_0}, to_apply=%region_0.0 | reduce-window | flops 1820672 | bytes 114692 | tf_op jit(solution)/shard_map/reduce-window
  12.3 0.1 slice.14
  12.4 0.2 copy.15
  12.5 0.1 add_bitcast_fusion
  12.7 0.7 multiply_reduce_fusion.1
  13.5 0.8 and_reduce_fusion
  14.2 0.1 reshape.362
  14.3 0.1 reshape.364
  14.4 8.8 %scatter_custom_fusion.1 = s32[2560]{0:T(1024)S(1)} fusion(s32[1600]{0:T(1024)S(1)} %reshape.362, s32[1600]{0:T(1024)S(1)} %reshape.364, s32[]{:T(128)} %constant.33.clone.1), kind=kCustom, calls=%fused_computation.54 | custom fusion | bytes 10244
  23.2 0.1 reshape.346
  23.3 0.1 all_to_all.18
  23.4 13.6 %all_to_all.21 = s32[8,1,320]{2,1,0:T(1,128)S(1)} all-to-all(s32[8,1,320]{2,1,0:T(1,128)S(1)} %all_to_all.18), channel_id=1, replica_groups=mesh['groups'=2,'rows'=8,'cols'=2] {'rows'}, dimensions={0} | all-to-all | bytes 20480 | tf_op jit(solution)/shard_map/all_to_all | solution.py:72
  37.1 0.1 reshape.350
  37.2 10.5 %gather_fusion = bf16[2560,512]{1,0:T(8,128)(2,1)} fusion(f32[2048,512]{1,0:T(8,128)} %param.7, s32[3072]{0:T(1024)S(1)} %pad_clamp_fusion), kind=kCustom, calls=%fused_computation | custom fusion | bytes 5253120 | tf_op jit(solution)/shard_map/jit(_take)/gather | solution.py:70
  47.7 3.2 %select_convert_fusion = bf16[8,320,512]{2,1,0:T(8,128)(2,1)} fusion(bf16[8,320,512]{2,1,0:T(8,128)(2,1)} %bitcast.25, pred[8,320]{1,0:T(8,128)(4,1)S(1)} %compare_and_fusion), kind=kLoop, calls=%fused_computation.3 | loop fusion | flops 1310720 | bytes 5245440 | tf_op jit(solution)/shard_map/convert_element_type | solution.py:76
  50.9 0.0 copy-start.2
  50.9 0.0 copy-start.4
  50.9 0.0 copy-start.7
  50.9 0.0 copy-start.6
  50.9 0.0 copy-start.3
  50.9 4.5 %all-to-all-start.1 = ((bf16[8,320,512]{2,1,0:T(8,128)(2,1)}), bf16[8,320,512]{2,1,0:T(8,128)(2,1)}, u32[]{:S(2)}, u32[]{:S(2)}) async-start(bf16[8,320,512]{2,1,0:T(8,128)(2,1)} %select_convert_fusion), calls=%async_computation.1 | async-start | bytes 5242880 | tf_op jit(solution)/shard_map/all_to_all | solution.py:75
  55.5 0.0 all-reduce.3.cloned.1.call-start
  55.5 0.1 reduce_sum.32
  55.6 0.0 copy-done.2
  55.6 0.1 reshape_reshape.7
  55.8 0.1 broadcast_add_fusion
  55.8 0.1 add.183
  55.9 0.1 add.186
  56.0 0.1 add.187
  56.1 0.0 copy-done.4
  56.1 0.1 reduce_sum.33
  56.2 0.1 broadcast_divide_fusion
  56.3 0.1 reshape.358
  56.4 0.1 compare_select_fusion.1
  56.5 0.0 copy-done.7
  56.5 0.1 multiply_reduce_fusion.2
  56.6 0.0 copy-done.6
  56.6 0.0 copy-start.1
  56.6 0.1 and_reduce_fusion.1
  56.7 10.1 %scatter_custom_fusion = f32[81920]{0:T(1024)S(1)} fusion(s32[1600]{0:T(1024)S(1)} %broadcast_select_fusion, f32[1600]{0:T(1024)S(1)} %reshape.358, f32[]{:T(128)} %constant.24.clone.1), kind=kCustom, calls=%fused_computation.6 | custom fusion | flops 1600 | bytes 327684
  66.8 0.1 reshape.342
  66.9 0.0 copy-done
  66.9 0.0 copy-done.3
  66.9 0.0 copy-start.5
  66.9 0.3 fusion.4
  67.2 46.6 %all-to-all-done.1 = bf16[8,320,512]{2,1,0:T(8,128)(2,1)} async-done(((bf16[8,320,512]{2,1,0:T(8,128)(2,1)}), bf16[8,320,512]{2,1,0:T(8,128)(2,1)}, u32[]{:S(2)}, u32[]{:S(2)}) %all-to-all-start.1) | async-done | bytes 2621472 | tf_op jit(solution)/shard_map/all_to_all | solution.py:75
  113.8 3.1 %convolution_convert_fusion = bf16[32,512]{1,0:T(8,128)(2,1)S(1)} fusion(f32[32,2560]{1,0:T(8,128)S(1)} %reshape.342, bf16[2560,512]{1,0:T(8,128)(2,1)} %bitcast.8), kind=kOutput, calls=%fused_computation.5 | convolution fusion | flops 503332864 | bytes 2981888 | tf_op jit(solution)/shard_map/dot_general | solution.py:78
  116.9 0.0 copy-done.1
  116.9 0.9 convolution_add_fusion
  117.8 0.0 all-reduce.3.cloned.1.call-update
  117.9 17.1 %all-reduce.3.cloned.1.call-done = f32[32,1024]{1,0:T(8,128)} async-done(((f32[32,1024]{1,0:T(8,128)}), f32[32,1024]{1,0:T(8,128)}) %all-reduce.3.cloned.1.call-update) | async-done | bytes 131088 | tf_op jit(solution)/shard_map/psum | solution.py:88
  135.0 0.0 copy-done.5
  135.0 1.0 multiply_reduce_fusion
  136.0 0.7 dynamic-slice_multiply_fusion
  (19 shorter events, 0.2 us)
Async XLA Ops:
  6.5 60.3 %copy-start = (bf16[512,1024]{1,0:T(8,128)(2,1)S(1)}, bf16[512,1024]{1,0:T(8,128)(2,1)}, u32[]{:S(2)}) copy-start(bf16[512,1024]{1,0:T(8,128)(2,1)} %param.11) | copy-start | bytes 3145732
  50.9 4.7 %copy-start.2 = (s32[32,50]{1,0:T(8,128)S(1)}, s32[32,50]{1,0:T(8,128)}, u32[]{:S(2)}) copy-start(s32[32,50]{1,0:T(8,128)} %param.9) | copy-start | bytes 19204
  50.9 5.2 %copy-start.4 = (f32[32,50]{1,0:T(8,128)S(1)}, f32[32,50]{1,0:T(8,128)}, u32[]{:S(2)}) copy-start(f32[32,50]{1,0:T(8,128)} %param.10) | copy-start | bytes 19204
  50.9 5.5 %copy-start.7 = (s32[2]{0:T(128)S(1)}, s32[2]{0:T(128)}, u32[]{:S(2)}) copy-start(s32[2]{0:T(128)} %constant.81) | copy-start | bytes 28
  50.9 5.6 %copy-start.6 = (s32[2]{0:T(128)S(1)}, s32[2]{0:T(128)}, u32[]{:S(2)}) copy-start(s32[2]{0:T(128)} %constant.84) | copy-start | bytes 28
  50.9 15.9 %copy-start.3 = (f32[32,512]{1,0:T(8,128)S(1)}, f32[32,512]{1,0:T(8,128)}, u32[]{:S(2)}) copy-start(f32[32,512]{1,0:T(8,128)} %param.8) | copy-start | bytes 196612
  50.9 62.9 %all-to-all-start.1 = ((bf16[8,320,512]{2,1,0:T(8,128)(2,1)}), bf16[8,320,512]{2,1,0:T(8,128)(2,1)}, u32[]{:S(2)}, u32[]{:S(2)}) async-start(bf16[8,320,512]{2,1,0:T(8,128)(2,1)} %select_convert_fusion), calls=%async_computation.1 | async-start | bytes 5242880 | tf_op jit(solution)/shard_map/all_to_all | solution.py:75
  55.5 79.5 %all-reduce.3.cloned.1.call-start = ((), (), s32[]{:S(2)}) async-start(), calls=%async_computation.2 | async-start | bytes 262144 | tf_op jit(solution)/shard_map/psum | solution.py:88
  56.6 60.3 %copy-start.1 = (bf16[512,1024]{1,0:T(8,128)(2,1)S(1)}, bf16[512,1024]{1,0:T(8,128)(2,1)}, u32[]{:S(2)}) copy-start(bf16[512,1024]{1,0:T(8,128)(2,1)} %param.12) | copy-start | bytes 3145732
  66.9 68.1 %copy-start.5 = (f32[1024]{0:T(1024)S(1)}, f32[1024]{0:T(1024)}, u32[]{:S(2)}) copy-start(f32[1024]{0:T(1024)} %param.13) | copy-start | bytes 12292
Sparse Core Ops, SparseCore 0:
  118.0 16.9 all-reduce.2
where the time goes:
time: 144 us
  waiting for transfers between devices  63.8 us (44%)
  local copies, waits for them, and re-layouts  22.4 us (16%)
  other arithmetic  21.3 us (15%)
  blocking collectives  13.6 us (9%)
  between operations  13.6 us (9%)
  starting transfers between devices  4.58 us (3%)
  matrix products  4.29 us (3%)
    all_to_all x1, waiting for transfers between devices, body(): lax.all_to_all(found.astype(jnp.bfloat16), 'rows', split_axis=0, concat_a...  46.6 us
    psum x1, waiting for transfers between devices, body(): preact = lax.psum(partial_sums, 'cols') + bias  17.1 us
    all_to_all x1, blocking collectives, body(): lax.all_to_all(outgoing, 'rows', split_axis=0, concat_axis=0, tiled=True)  13.6 us
    unnamed x7, other arithmetic  11.8 us
    gather x1, local copies, waits for them, and re-layouts, body(): jnp.take(feature_table, lax.all_to_all(outgoing, 'rows', split_axis=0, co...  10.5 us
    unnamed x19, local copies, waits for them, and re-layouts  8.94 us
    all_to_all x1, starting transfers between devices, body(): lax.all_to_all(found.astype(jnp.bfloat16), 'rows', split_axis=0, concat_a...  4.54 us
    another operation x4, other arithmetic  4.06 us
  transfers between devices with their start and end apart: 2, of which 2 were waited for; matrix products, arithmetic and copies ran while one was open for 8% of the time, Pallas kernels for 0%

commit v1 on v0

--- a/solution.py
+++ b/solution.py
@@ -6,6 +6,11 @@
 
 NEIGH = 50
 TGT_DEV = 16
+
+
+def summed_here(x, mesh_axis):
+    pieces = lax.all_gather(x, mesh_axis)
+    return jnp.sum(pieces, axis=0)
 
 
 def request_slots(id_block, share_block, owners, capacity, rows_dev):
@@ -85,7 +90,7 @@
         pooled.astype(jnp.bfloat16), w_pool, preferred_element_type=jnp.float32
     )
     column_start = lax.axis_index("cols") * width_half
-    preact = lax.psum(partial_sums, "cols") + bias
+    preact = summed_here(partial_sums, "cols") + bias
     embedded = finish_rows(preact)
     return lax.dynamic_slice_in_dim(embedded, column_start, width_half, 1)
 

time: 144 us -> 114 us (0.79)
  waiting for transfers between devices: 63.8 us -> 46.7 us
  between operations: 13.6 us -> 0.26 us
  blocking collectives: 13.6 us -> 15.6 us
    psum x1 -> x0, waiting for transfers between devices: 17.1 us -> none  [body(): preact = lax.psum(partial_sums, 'cols') + bias]
    all_gather x0 -> x1, blocking collectives: none -> 1.99 us  [summed_here(): pieces = lax.all_gather(x, mesh_axis)]
  transfers between devices with their start and end apart: 2 -> 1, of which waited for: 2 -> 1; matrix products, arithmetic and copies ran while one was open for 8% -> 10% of each run, Pallas kernels for 0% -> 0%
where the time goes in v1:
time: 114 us
  waiting for transfers between devices  46.7 us (41%)
  local copies, waits for them, and re-layouts  22.3 us (20%)
  other arithmetic  20.4 us (18%)
  blocking collectives  15.6 us (14%)
  starting transfers between devices  4.54 us (4%)
  matrix products  3.63 us (3%)
    all_to_all x1, waiting for transfers between devices, body(): lax.all_to_all(found.astype(jnp.bfloat16), 'rows', split_axis=0, concat_a...  46.7 us
    all_to_all x1, blocking collectives, body(): lax.all_to_all(outgoing, 'rows', split_axis=0, concat_axis=0, tiled=True)  13.6 us
    unnamed x7, other arithmetic  11.8 us
    gather x1, local copies, waits for them, and re-layouts, body(): jnp.take(feature_table, lax.all_to_all(outgoing, 'rows', split_axis=0, co...  10.5 us
    unnamed x19, local copies, waits for them, and re-layouts  8.93 us
    all_to_all x1, starting transfers between devices, body(): lax.all_to_all(found.astype(jnp.bfloat16), 'rows', split_axis=0, concat_a...  4.54 us
    another operation x4, other arithmetic  4.06 us
    convert_element_type x1, other arithmetic, body(): found.astype(jnp.bfloat16)  3.2 us
  transfers between devices with their start and end apart: 1, of which 1 were waited for; matrix products, arithmetic and copies ran while one was open for 10% of the time, Pallas kernels for 0%

profile of v1, /device:TPU:0, one launch (start us, length us, event | category | flops | bytes accessed | tf_op | source)
XLA Modules:
  0.0 113.5 jit_solution(12359786787237328707)
XLA Ops:
  0.0 0.0 copy-start
  0.0 0.9 reshape_reshape.8
  0.9 0.8 reshape_reshape.9
  1.8 4.0 %reduce-window.6 = s32[2,8,7,128]{3,1,2,0:T(8,128)S(1)} reduce-window(s32[2,8,7,128]{3,1,2,0:T(8,128)S(1)} %convert_bitcast_fusion, s32[]{:T(128)} %constant.33.clone.1), window={size=1x1x1x128 pad=0_0x0_0x0_0x127_0}, to_apply=%region_0.0 | reduce-window | flops 1820672 | bytes 114692 | tf_op jit(solution)/shard_map/reduce-window
  5.7 0.1 slice.14
  5.8 0.2 copy.15
  6.0 0.1 add_bitcast_fusion
  6.2 0.7 multiply_reduce_fusion.1
  6.9 0.8 and_reduce_fusion
  7.7 0.1 reshape.362
  7.8 0.1 reshape.364
  7.9 8.8 %scatter_custom_fusion.1 = s32[2560]{0:T(1024)S(1)} fusion(s32[1600]{0:T(1024)S(1)} %reshape.362, s32[1600]{0:T(1024)S(1)} %reshape.364, s32[]{:T(128)} %constant.33.clone.1), kind=kCustom, calls=%fused_computation.54 | custom fusion | bytes 10244
  16.7 0.1 reshape.346
  16.8 0.1 all_to_all.18
  16.9 13.6 %all_to_all.21 = s32[8,1,320]{2,1,0:T(1,128)S(1)} all-to-all(s32[8,1,320]{2,1,0:T(1,128)S(1)} %all_to_all.18), channel_id=1, replica_groups=mesh['groups'=2,'rows'=8,'cols'=2] {'rows'}, dimensions={0} | all-to-all | bytes 20480 | tf_op jit(solution)/shard_map/all_to_all | solution.py:77
  30.6 0.1 reshape.350
  30.6 10.5 %gather_fusion = bf16[2560,512]{1,0:T(8,128)(2,1)} fusion(f32[2048,512]{1,0:T(8,128)} %param.7, s32[3072]{0:T(1024)S(1)} %pad_clamp_fusion), kind=kCustom, calls=%fused_computation | custom fusion | bytes 5253120 | tf_op jit(solution)/shard_map/jit(_take)/gather | solution.py:75
  41.2 3.2 %select_convert_fusion = bf16[8,320,512]{2,1,0:T(8,128)(2,1)} fusion(bf16[8,320,512]{2,1,0:T(8,128)(2,1)} %bitcast.26, pred[8,320]{1,0:T(8,128)(4,1)S(1)} %compare_and_fusion), kind=kLoop, calls=%fused_computation.3 | loop fusion | flops 1310720 | bytes 5245440 | tf_op jit(solution)/shard_map/convert_element_type | solution.py:81
  44.4 0.0 copy-start.2
  44.4 0.0 copy-start.4
  44.4 0.0 copy-start.7
  44.4 0.0 copy-start.6
  44.4 0.0 copy-start.3
  44.4 4.5 %all-to-all-start.1 = ((bf16[8,320,512]{2,1,0:T(8,128)(2,1)}), bf16[8,320,512]{2,1,0:T(8,128)(2,1)}, u32[]{:S(2)}, u32[]{:S(2)}) async-start(bf16[8,320,512]{2,1,0:T(8,128)(2,1)} %select_convert_fusion), calls=%async_computation.1 | async-start | bytes 5242880 | tf_op jit(solution)/shard_map/all_to_all | solution.py:80
  49.0 0.1 reduce_sum.41
  49.0 0.0 copy-done.2
  49.0 0.1 reshape_reshape.7
  49.2 0.1 broadcast_add_fusion
  49.3 0.1 add.181
  49.4 0.1 add.184
  49.4 0.1 add.185
  49.5 0.0 copy-done.4
  49.5 0.1 reduce_sum.42
  49.6 0.1 broadcast_divide_fusion
  49.7 0.1 reshape.358
  49.8 0.1 compare_select_fusion.1
  49.9 0.0 copy-done.7
  49.9 0.1 multiply_reduce_fusion.2
  50.0 0.0 copy-done.6
  50.0 0.1 and_reduce_fusion.1
  50.1 0.0 copy-start.1
  50.1 10.1 %scatter_custom_fusion = f32[81920]{0:T(1024)S(1)} fusion(s32[1600]{0:T(1024)S(1)} %broadcast_select_fusion, f32[1600]{0:T(1024)S(1)} %reshape.358, f32[]{:T(128)} %constant.24.clone.1), kind=kCustom, calls=%fused_computation.6 | custom fusion | flops 1600 | bytes 327684
  60.2 0.1 reshape.342
  60.3 0.0 copy-done
  60.3 0.0 copy-done.3
  60.3 0.3 fusion.4
  60.6 0.0 copy-start.5
  60.6 46.7 %all-to-all-done.1 = bf16[8,320,512]{2,1,0:T(8,128)(2,1)} async-done(((bf16[8,320,512]{2,1,0:T(8,128)(2,1)}), bf16[8,320,512]{2,1,0:T(8,128)(2,1)}, u32[]{:S(2)}, u32[]{:S(2)}) %all-to-all-start.1) | async-done | bytes 2621472 | tf_op jit(solution)/shard_map/all_to_all | solution.py:80
  107.3 3.1 %convolution_convert_fusion = bf16[32,512]{1,0:T(8,128)(2,1)S(1)} fusion(f32[32,2560]{1,0:T(8,128)S(1)} %reshape.342, bf16[2560,512]{1,0:T(8,128)(2,1)} %bitcast.8), kind=kOutput, calls=%fused_computation.5 | convolution fusion | flops 503332864 | bytes 2981888 | tf_op jit(solution)/shard_map/dot_general | solution.py:83
  110.3 0.0 copy-done.1
  110.4 0.3 convolution_add_fusion
  110.6 2.0 %all-gather = f32[64,1024]{1,0:T(8,128)S(1)} all-gather(f32[32,1024]{1,0:T(8,128)S(1)} %convolution_add_fusion), channel_id=2, replica_groups=mesh['groups'=2,'rows'=8,'cols'=2] {'cols'}, dimensions={0}, use_global_device_ids=true | all-gather | bytes 393216 | tf_op jit(solution)/shard_map/all_gather | solution.py:12
  112.7 0.0 copy-done.5
  112.7 0.1 multiply_reduce_fusion
  112.8 0.7 dynamic-slice_multiply_fusion
  (20 shorter events, 0.3 us)
Async XLA Ops:
  0.0 60.3 %copy-start = (bf16[512,1024]{1,0:T(8,128)(2,1)S(1)}, bf16[512,1024]{1,0:T(8,128)(2,1)}, u32[]{:S(2)}) copy-start(bf16[512,1024]{1,0:T(8,128)(2,1)} %param.11) | copy-start | bytes 3145732
  44.4 4.7 %copy-start.2 = (s32[32,50]{1,0:T(8,128)S(1)}, s32[32,50]{1,0:T(8,128)}, u32[]{:S(2)}) copy-start(s32[32,50]{1,0:T(8,128)} %param.9) | copy-start | bytes 19204
  44.4 5.1 %copy-start.4 = (f32[32,50]{1,0:T(8,128)S(1)}, f32[32,50]{1,0:T(8,128)}, u32[]{:S(2)}) copy-start(f32[32,50]{1,0:T(8,128)} %param.10) | copy-start | bytes 19204
  44.4 5.5 %copy-start.7 = (s32[2]{0:T(128)S(1)}, s32[2]{0:T(128)}, u32[]{:S(2)}) copy-start(s32[2]{0:T(128)} %constant.81) | copy-start | bytes 28
  44.4 5.6 %copy-start.6 = (s32[2]{0:T(128)S(1)}, s32[2]{0:T(128)}, u32[]{:S(2)}) copy-start(s32[2]{0:T(128)} %constant.84) | copy-start | bytes 28
  44.4 15.9 %copy-start.3 = (f32[32,512]{1,0:T(8,128)S(1)}, f32[32,512]{1,0:T(8,128)}, u32[]{:S(2)}) copy-start(f32[32,512]{1,0:T(8,128)} %param.8) | copy-start | bytes 196612
  44.4 62.9 %all-to-all-start.1 = ((bf16[8,320,512]{2,1,0:T(8,128)(2,1)}), bf16[8,320,512]{2,1,0:T(8,128)(2,1)}, u32[]{:S(2)}, u32[]{:S(2)}) async-start(bf16[8,320,512]{2,1,0:T(8,128)(2,1)} %select_convert_fusion), calls=%async_computation.1 | async-start | bytes 5242880 | tf_op jit(solution)/shard_map/all_to_all | solution.py:80
  50.1 60.2 %copy-start.1 = (bf16[512,1024]{1,0:T(8,128)(2,1)S(1)}, bf16[512,1024]{1,0:T(8,128)(2,1)}, u32[]{:S(2)}) copy-start(bf16[512,1024]{1,0:T(8,128)(2,1)} %param.12) | copy-start | bytes 3145732
  60.6 52.1 %copy-start.5 = (f32[1024]{0:T(1024)S(1)}, f32[1024]{0:T(1024)}, u32[]{:S(2)}) copy-start(f32[1024]{0:T(1024)} %param.13) | copy-start | bytes 12292
